TPU v7x, 64 devices: a 2x2x8 block of a 4x4x8 slice. The times are simulated.
64 devices in a mesh: dp: 4 (over x, y), dcp: 16 (over z, core).
Axes of the slice: x: 2, y: 2, z: 8, core: 2. Of those that a mesh axis runs over, the one named last changes fastest.
The devices are a block of a 4x4x8 slice.
Arguments:
- q_abs: bfloat16 [64, 128, 576], P('dp', 'dcp'), parts along dimension 0
- cache: bfloat16 [64, 16384, 576], P('dp', 'dcp'), parts along dimension 0
- lengths: int32 [64], P('dp'), parts along dimension 0
Outputs:
- output: bfloat16 [64, 128, 512], P('dp', 'dcp'), parts along dimension 0
There are 4 independent parts. A program takes and returns all parts, laid end to end along the dimension named above; each array names one.
All inputs are finite; a program needn't handle non-finite values.
Results may differ from a plain program's by a relative error of at most 0.00794391.
Values are sent between devices in bfloat16 or wider.
A program may use at most 768 MiB of HBM per device.

v0:
```python
import jax
import jax.numpy as jnp
from jax import lax
from jax.sharding import PartitionSpec as P

ROPE = 64
SCALE = 192 ** -0.5


def partial_attention(q, blk, valid, lat):
    s = jnp.einsum('bhk,btk->bht', q, blk, preferred_element_type=jnp.float32) * SCALE
    s = jnp.where(valid[:, None, :], s, -jnp.inf)
    m = jnp.max(s, axis=2)
    m0 = jnp.where(jnp.isfinite(m), m, 0.0)
    p = jnp.exp(s - m0[:, :, None])
    l = jnp.sum(p, axis=2)
    pv = jnp.einsum('bht,btc->bhc', p.astype(jnp.bfloat16), blk[:, :, :lat], preferred_element_type=jnp.float32)
    has = l > 0.0
    l1 = jnp.where(has, l, 1.0)
    od = (pv / l1[:, :, None]).astype(jnp.bfloat16)
    lse = jnp.where(has, m0 + jnp.log(l1), -jnp.inf)
    return od, lse


def merge(od, lse, axis):
    mx = jnp.max(lse, axis=axis, keepdims=True)
    wt = jnp.exp(lse - mx)
    wt = wt / jnp.sum(wt, axis=axis, keepdims=True)
    return jnp.sum(wt[..., None] * od.astype(jnp.float32), axis=axis).astype(jnp.bfloat16)


def solution(mesh):
    n = mesh.shape['dcp']

    def local(q, cache, lengths):
        d = lax.axis_index('dcp')
        b, sl, wd = cache.shape
        lat = wd - ROPE
        qa = lax.all_gather(q, 'dcp', axis=1, tiled=True)
        pos = d * sl + jnp.arange(sl)
        valid = pos[None, :] < lengths[:, None]
        od, lse = partial_attention(qa, cache, valid, lat)
        h = od.shape[1]
        od = od.reshape(b, n, h // n, lat)
        lse = lse.reshape(b, n, h // n)
        od = lax.all_to_all(od, 'dcp', 1, 1, tiled=True)
        lse = lax.all_to_all(lse, 'dcp', 1, 1, tiled=True)
        return merge(od, lse, 1)

    return jax.shard_map(local, mesh=mesh, in_specs=(P('dp', 'dcp', None), P('dp', 'dcp', None), P('dp')), out_specs=P('dp', 'dcp', None), check_vma=False)
```

profile of v0, /device:TPU:21, one launch (start us, length us, event | category | flops | bytes accessed | tf_op | source)
XLA Modules:
  0.0 151.9 jit_solution(1280436470712079937)
XLA Ops:
  6.5 0.0 all-gather.2.cloned.1.call-start
  6.6 0.7 all-gather.2.cloned.1.call-update
  7.3 0.7 broadcast_compare_fusion
  8.1 42.6 %all-gather.2.cloned.1.call-done = bf16[16,128,576]{2,1,0:T(8,128)(2,1)} async-done(((bf16[16,8,576]{2,1,0:T(8,128)(2,1)}), bf16[16,128,576]{2,1,0:T(8,128)(2,1)}) %all-gather.2.cloned.1.call-update) | async-done | bytes 2359312 | tf_op jit(solution)/shard_map/all_gather | solution.py:39
  50.7 14.2 %fusion.2 = (f32[16,128]{1,0:T(8,128)S(1)}, f32[16,128,1024]{2,1,0:T(8,128)}) fusion(pred[16,1024]{1,0:T(8,128)(4,1)S(1)} %broadcast_compare_fusion, bf16[16,128,576]{2,1,0:T(8,128)(2,1)} %all-gather.2.cloned.1.call-done, bf16[16,1024,576]{1,2,0:T(8,128)(2,1)} %param.4), kind=kOutput, calls=%fused_computation.4 | convolution fusion | flops 2422208512 | bytes 29646848 | tf_op jit(solution)/shard_map/bhk,btk->bht/dot_general | solution.py:11
  64.9 0.1 copy.10
  65.0 4.5 %fusion.4 = f32[16,128]{1,0:T(8,128)S(1)} fusion(f32[16,128,1024]{2,1,0:T(8,128)} %get-tuple-element.6, f32[16,128]{1,0:T(8,128)S(1)} %is-finite_select_fusion.1, pred[16,1024]{1,0:T(8,128)(4,1)S(1)} %broadcast_compare_fusion), kind=kLoop, calls=%fused_computation.6 | loop fusion | flops 8386560 | bytes 8421376 | tf_op jit(solution)/shard_map/reduce_sum | solution.py:16
  69.6 0.1 copy.9
  69.7 0.7 reshape.45
  70.4 4.6 %all-to-all-start = ((f32[16,1,128]{2,1,0:T(1,128)}), f32[16,1,128]{2,1,0:T(1,128)S(1)}, u32[]{:S(2)}, u32[]{:S(2)}) async-start(f32[16,1,128]{2,1,0:T(1,128)} %reshape.45), calls=%async_computation | async-start | bytes 16384 | tf_op jit(solution)/shard_map/all_to_all | solution.py:47
  75.0 11.2 %fusion.10 = bf16[16,16,8,512]{3,2,1,0:T(8,128)(2,1)S(1)} fusion(f32[16,128]{1,0:T(8,128)S(1)} %compare_select_fusion.2, bf16[16,1024,576]{1,2,0:T(8,128)(2,1)} %param.4, f32[16,128,1024]{2,1,0:T(8,128)} %get-tuple-element.6, f32[16,128]{1,0:T(8,128)S(1)} %is-finite_select_fusion.1, pred[16,1024]{1,0:T(8,128)(4,1)S(1)} %broadcast_compare_fusion), kind=kOutput, calls=%fused_computation.13 | convolution fusion | flops 2157969408 | bytes 27295744 | tf_op jit(solution)/shard_map/bht,btc->bhc/dot_general | solution.py:17
  86.3 1.6 %copy.13 = bf16[16,16,8,512]{3,2,0,1:T(8,128)(2,1)} copy(bf16[16,16,8,512]{3,2,1,0:T(8,128)(2,1)S(1)} %fusion.10) | data formatting | bytes 4194304 | tf_op jit(solution)/shard_map/reshape | solution.py:44
  87.8 0.0 all-to-all-done
  87.8 7.2 %all-to-all-start.1 = ((bf16[16,16,8,512]{3,2,0,1:T(8,128)(2,1)}), bf16[16,16,8,512]{3,2,0,1:T(8,128)(2,1)S(1)}, u32[]{:S(2)}, u32[]{:S(2)}) async-start(bf16[16,16,8,512]{3,2,0,1:T(8,128)(2,1)} %copy.13), calls=%async_computation.1 | async-start | bytes 4194304 | tf_op jit(solution)/shard_map/all_to_all | solution.py:46
  95.1 0.5 broadcast.38
  95.6 0.7 reduce
  96.3 0.1 reshape.46
  96.4 0.1 copy.11
  96.5 47.4 %all-to-all-done.1 = bf16[16,16,8,512]{3,2,0,1:T(8,128)(2,1)S(1)} async-done(((bf16[16,16,8,512]{3,2,0,1:T(8,128)(2,1)}), bf16[16,16,8,512]{3,2,0,1:T(8,128)(2,1)S(1)}, u32[]{:S(2)}, u32[]{:S(2)}) %all-to-all-start.1) | async-done | bytes 2097184 | tf_op jit(solution)/shard_map/all_to_all | solution.py:46
  143.9 1.1 multiply_reduce_fusion
  (7 shorter events, 0.1 us)
Async XLA Ops:
  6.5 44.2 %all-gather.2.cloned.1.call-start = ((), (), s32[]{:S(2)}) async-start(), calls=%async_computation.2 | async-start | bytes 2785280 | tf_op jit(solution)/shard_map/all_gather | solution.py:39
  70.4 17.4 %all-to-all-start = ((f32[16,1,128]{2,1,0:T(1,128)}), f32[16,1,128]{2,1,0:T(1,128)S(1)}, u32[]{:S(2)}, u32[]{:S(2)}) async-start(f32[16,1,128]{2,1,0:T(1,128)} %reshape.45), calls=%async_computation | async-start | bytes 16384 | tf_op jit(solution)/shard_map/all_to_all | solution.py:47
  87.8 56.0 %all-to-all-start.1 = ((bf16[16,16,8,512]{3,2,0,1:T(8,128)(2,1)}), bf16[16,16,8,512]{3,2,0,1:T(8,128)(2,1)S(1)}, u32[]{:S(2)}, u32[]{:S(2)}) async-start(bf16[16,16,8,512]{3,2,0,1:T(8,128)(2,1)} %copy.13), calls=%async_computation.1 | async-start | bytes 4194304 | tf_op jit(solution)/shard_map/all_to_all | solution.py:46
Sparse Core Ops, SparseCore 0:
  8.9 41.7 all-gather.1
where the time goes:
time: 152 us
  waiting for transfers between devices  90.7 us (60%)
  matrix products  25.5 us (17%)
  between operations  13.5 us (9%)
  starting transfers between devices  11.8 us (8%)
  other arithmetic  7.17 us (5%)
  local copies, waits for them, and re-layouts  3.14 us (2%)
    all_to_all x1, waiting for transfers between devices, local(): od = lax.all_to_all(od, 'dcp', 1, 1, tiled=True)  47.4 us
    all_gather x1, waiting for transfers between devices, local(): qa = lax.all_gather(q, 'dcp', axis=1, tiled=True)  42.6 us
    dot_general x1, matrix products, partial_attention(): jnp.einsum('bhk,btk->bht', q, blk, preferred_element_type=jnp.float32)  14.2 us
    dot_general x1, matrix products, partial_attention(): jnp.einsum('bht,btc->bhc', p.astype(jnp.bfloat16), blk[:, :, :lat], prefe...  11.2 us
    all_to_all x1, starting transfers between devices, local(): od = lax.all_to_all(od, 'dcp', 1, 1, tiled=True)  7.24 us
    all_to_all x1, starting transfers between devices, local(): lse = lax.all_to_all(lse, 'dcp', 1, 1, tiled=True)  4.6 us
    reduce_sum x1, other arithmetic, partial_attention(): l = jnp.sum(p, axis=2)  4.54 us
  transfers between devices with their start and end apart: 3, of which 2 were waited for; matrix products, arithmetic and copies ran while one was open for 10% of the time, Pallas kernels for 0%

commit v1 on v0

v1 whole, which is shorter than its diff:
```python
import functools

import jax
import jax.numpy as jnp
from jax import lax
from jax.experimental import pallas as pl
from jax.experimental.pallas import tpu as pltpu
from jax.sharding import PartitionSpec as P

ROPE = 64
SCALE = 192 ** -0.5
PAIR = 2
PIECE = 4
SKEW = 2
LANES = 128


def weights(lse):
    m = functools.reduce(jnp.maximum, lse)
    m = jnp.where(m == -jnp.inf, 0.0, m)
    w = [jnp.exp(x - m) for x in lse]
    t = functools.reduce(jnp.add, w)
    has = t > 0.0
    t1 = jnp.where(has, t, 1.0)
    inv = 1.0 / t1
    return [x * inv for x in w], jnp.where(has, m + jnp.log(t1), -jnp.inf)


def blend(parts, ws):
    reps = parts[0].shape[1] // LANES
    return functools.reduce(jnp.add, [x * jnp.concatenate([w] * reps, axis=1) for x, w in zip(parts, ws)])


def kernel(n, len_ref, q_ref, ct_ref, o_ref, ct, qall, own, sout, sin, lbuf, sbuf,
           csem, qsem, ags, agr, ds, dr, xs, xr, ls, lr, ss, sr):
    me = lax.axis_index('dcp')
    z, core = me // 2, me % 2
    chips = n // 2
    far, near = chips // 2, chips - 1 - chips // 2
    b, hl, wd = q_ref.shape
    sl = ct_ref.shape[2]
    lat = wd - ROPE
    groups, pieces = b // PAIR, b // PIECE
    rows = chips * hl

    def dev(off):
        return {'dcp': lax.rem(z + off + chips, chips) * 2 + core}

    sib = {'dcp': z * 2 + 1 - core}

    def remote(src, dst, s, r, to):
        return pltpu.make_async_remote_copy(src, dst, s, r, device_id=to, device_id_type=pl.DeviceIdType.MESH)

    qcopy = pltpu.make_async_copy(q_ref, qall.at[0, 0], qsem)
    qcopy.start()

    def cache_copy(s):
        return pltpu.make_async_copy(ct_ref.at[s], ct.at[s], csem.at[s])

    @pl.loop(0, b)
    def _(s):
        cache_copy(s).start()

    bar = pltpu.get_barrier_semaphore()
    for to in (dev(1), dev(-1), sib):
        pl.semaphore_signal(bar, inc=1, device_id=to, device_id_type=pl.DeviceIdType.MESH)
    pl.semaphore_wait(bar, 3)
    qcopy.wait()

    def q_at(half, r, p):
        return qall.at[half, r % chips, pl.ds(p * PIECE, PIECE)]

    def ring_q(p, k, long):
        sg = 1 if (p % 2 == 0) == long else -1
        i = k if long else far + k
        return remote(q_at(0, -k * sg, p), q_at(0, -(k + 1) * sg, p), ags.at[p, i], agr.at[p, i], dev(sg))

    def sib_q(p, r):
        return remote(q_at(0, r, p), q_at(1, r, p), ds.at[p, r % chips], dr.at[p, r % chips], sib)

    for p in range(pieces):
        ring_q(p, 0, True).start()
        ring_q(p, 0, False).start()
    for p in range(pieces):
        sib_q(p, 0).start()
    for k in range(1, far + 1):
        for p in range(pieces):
            for long in (True, False):
                hops = far if long else near
                if k <= hops:
                    sg = 1 if (p % 2 == 0) == long else -1
                    ring_q(p, k - 1, long).wait_recv()
                    if k < hops:
                        ring_q(p, k, long).start()
                    sib_q(p, -k * sg).start()
    for p in range(pieces):
        for r in range(chips):
            sib_q(p, r).wait_recv()

    base = me * sl

    def attend(s):
        cache_copy(s).wait()
        q = qall[:, :, s].reshape(2 * chips, hl, wd).astype(jnp.float32).reshape(2 * rows, wd).astype(jnp.bfloat16)
        sc = jnp.dot(q, ct[s], preferred_element_type=jnp.float32) * SCALE
        pos = base + lax.broadcasted_iota(jnp.int32, sc.shape, 1)
        sc = jnp.where(pos < len_ref[s], sc, -jnp.inf)
        m = jnp.max(sc, axis=1, keepdims=True)
        m0 = jnp.where(m == -jnp.inf, 0.0, m)
        p = jnp.exp(sc - m0)
        l = jnp.sum(p, axis=1, keepdims=True)
        pv = lax.dot_general(p.astype(jnp.bfloat16), ct[s, pl.ds(0, lat)], (((1,), (1,)), ((), ())),
                             preferred_element_type=jnp.float32)
        has = l > 0.0
        l1 = jnp.where(has, l, 1.0)
        od = (pv / l1).astype(jnp.bfloat16).astype(jnp.float32)
        lse = jnp.broadcast_to(jnp.where(has, m0 + jnp.log(l1), -jnp.inf), (2 * rows, LANES))
        own[s, :, pl.ds(0, lat)] = od[:rows]
        own[s, :, pl.ds(lat, LANES)] = lse[:rows]
        sout[s, :, pl.ds(0, lat)] = od[rows:]
        sout[s, :, pl.ds(lat, LANES)] = lse[rows:]

    def swap(g):
        return remote(sout.at[pl.ds(g * PAIR, PAIR)], sin.at[pl.ds(g * PAIR, PAIR)], xs.at[g], xr.at[g], sib)

    lane = lax.broadcasted_iota(jnp.int32, (hl, LANES), 1)

    def sign(g, long):
        odd = lax.rem(g, 2)
        return 1 - 2 * odd if long else 2 * odd - 1

    def chain(g, k, long):
        buf, s, r = (lbuf, ls, lr) if long else (sbuf, ss, sr)
        return remote(buf.at[g, k], buf.at[g, k + 1], s.at[g, k], r.at[g, k], dev(sign(g, long)))

    def mine(g, a, r):
        at = pl.ds(pl.multiple_of(lax.rem(r + chips, chips) * hl, hl), hl)
        return own[g * PAIR + a, at, pl.ds(0, lat)], own[g * PAIR + a, at, pl.ds(lat, LANES)]

    def unpack(buf, g, k, a):
        t = buf[g, k, :, pl.ds(PAIR * lat, LANES)]
        c = a * (LANES // PAIR)
        return buf[g, k, :, pl.ds(a * lat, lat)], jnp.broadcast_to(t[:, c:c + 1], (hl, LANES))

    def put(buf, g, k, parts):
        for a in range(PAIR):
            buf[g, k, :, pl.ds(a * lat, lat)] = parts[a][0]
        buf[g, k, :, pl.ds(PAIR * lat, LANES)] = jnp.where(lane < LANES // PAIR, parts[0][1], parts[1][1])

    def begin(g):
        swap(g).wait_recv()
        for a in range(PAIR):
            s = g * PAIR + a
            w, lse = weights([own[s, :, pl.ds(lat, LANES)], sin[s, :, pl.ds(lat, LANES)]])
            own[s, :, pl.ds(0, lat)] = blend([own[s, :, pl.ds(0, lat)], sin[s, :, pl.ds(0, lat)]], w)
            own[s, :, pl.ds(lat, LANES)] = lse
        for long, buf, hops in ((True, lbuf, far), (False, sbuf, near)):
            put(buf, g, 0, [mine(g, a, hops * sign(g, long)) for a in range(PAIR)])
            chain(g, 0, long).start()

    def hop(g, k, long):
        buf, hops = (lbuf, far) if long else (sbuf, near)
        chain(g, k - 1, long).wait_recv()
        parts = []
        for a in range(PAIR):
            x, y = unpack(buf, g, k, a), mine(g, a, (hops - k) * sign(g, long))
            w, lse = weights([x[1], y[1]])
            parts.append((blend([x[0], y[0]], w), lse))
        put(buf, g, k, parts)
        chain(g, k, long).start()

    def finish(g):
        chain(g, far - 1, True).wait_recv()
        chain(g, near - 1, False).wait_recv()
        for a in range(PAIR):
            x, y, v = unpack(lbuf, g, far, a), unpack(sbuf, g, near, a), mine(g, a, 0)
            w, _ = weights([x[1], y[1], v[1]])
            o_ref[g * PAIR + a] = blend([x[0], y[0], v[0]], w).astype(o_ref.dtype)

    def when(g, f):
        @pl.when(jnp.logical_and(g >= 0, g < groups))
        def _():
            f(g)

    @pl.loop(0, groups + 1 + SKEW * far)
    def _(i):
        when(i, lambda g: attend(g * PAIR))
        when(i - 1, begin)

        def rest(g):
            for a in range(1, PAIR):
                attend(g * PAIR + a)
            swap(g).start()

        when(i, rest)
        when(i - 1 - SKEW * far, finish)
        for k in range(far - 1, 0, -1):
            def step(g, k=k):
                hop(g, k, True)
                if k < near:
                    hop(g, k, False)
            when(i - 1 - SKEW * k, step)

    for p in range(pieces):
        for k in range(far):
            ring_q(p, k, True).wait_send()
        for k in range(near):
            ring_q(p, k, False).wait_send()
        for r in range(chips):
            sib_q(p, r).wait_send()

    @pl.loop(0, groups)
    def _(g):
        swap(g).wait_send()
        for k in range(far):
            chain(g, k, True).wait_send()
        for k in range(near):
            chain(g, k, False).wait_send()


def solution(mesh):
    n = mesh.shape['dcp']

    def local(q, cache, lengths):
        b, sl, wd = cache.shape
        hl = q.shape[1]
        lat = wd - ROPE
        chips = n // 2
        far, near = chips // 2, chips - 1 - chips // 2
        groups, pieces = b // PAIR, b // PIECE
        rows = chips * hl
        dma = pltpu.SemaphoreType.DMA
        return pl.pallas_call(
            functools.partial(kernel, n),
            out_shape=jax.ShapeDtypeStruct((b, hl, lat), jnp.bfloat16),
            in_specs=[pl.BlockSpec(memory_space=pltpu.SMEM), pl.BlockSpec(memory_space=pl.ANY),
                      pl.BlockSpec(memory_space=pl.ANY)],
            out_specs=pl.BlockSpec(memory_space=pltpu.VMEM),
            scratch_shapes=[
                pltpu.VMEM((b, wd, sl), jnp.bfloat16),
                pltpu.VMEM((2, chips, b, hl, wd), jnp.bfloat16),
                pltpu.VMEM((b, rows, lat + LANES), jnp.float32),
                pltpu.VMEM((b, rows, lat + LANES), jnp.float32),
                pltpu.VMEM((b, rows, lat + LANES), jnp.float32),
                pltpu.VMEM((groups, far + 1, hl, PAIR * lat + LANES), jnp.float32),
                pltpu.VMEM((groups, near + 1, hl, PAIR * lat + LANES), jnp.float32),
                dma((b,)), dma,
                dma((pieces, far + near)), dma((pieces, far + near)),
                dma((pieces, chips)), dma((pieces, chips)),
                dma((groups,)), dma((groups,)),
                dma((groups, far)), dma((groups, far)),
                dma((groups, near)), dma((groups, near)),
            ],
            compiler_params=pltpu.CompilerParams(
                collective_id=0, has_side_effects=True, vmem_limit_bytes=60 * 1024 * 1024),
            name='mla_decode',
        )(lengths, q, jnp.swapaxes(cache, 1, 2))

    return jax.shard_map(local, mesh=mesh, in_specs=(P('dp', 'dcp', None), P('dp', 'dcp', None), P('dp')),
                         out_specs=P('dp', 'dcp', None), check_vma=False)
```

time: 152 us -> 66.7 us (0.44)
  waiting for transfers between devices: 90.7 us -> 0 us
  Pallas kernels: 0 us -> 64.1 us
  matrix products: 25.5 us -> 0 us
  between operations: 13.5 us -> 0.01 us
  starting transfers between devices: 11.8 us -> 0 us
  other arithmetic: 7.17 us -> 0 us
  local copies, waits for them, and re-layouts: 3.14 us -> 1.57 us
    pallas_call x0 -> x1, Pallas kernels: none -> 64.1 us  [local(): pl.pallas_call(functools.partial(kernel, n), out_shape=jax.ShapeDtypeStru...]
    all_to_all x2 -> x0, waiting for transfers between devices: 47.4 us -> none  [the longest x1 47.4 us: local(): od = lax.all_to_all(od, 'dcp', 1, 1, tiled=True)]
    all_gather x1 -> x0, waiting for transfers between devices: 42.6 us -> none  [local(): qa = lax.all_gather(q, 'dcp', axis=1, tiled=True)]
    dot_general x2 -> x0, matrix products: 25.5 us -> none  [the longest x1 14.2 us: partial_attention(): jnp.einsum('bhk,btk->bht', q, blk, preferred_element_type=jnp.float32)]
    all_to_all x2 -> x0, starting transfers between devices: 11.8 us -> none  [the longest x1 7.24 us: local(): od = lax.all_to_all(od, 'dcp', 1, 1, tiled=True)]
    reduce_sum x3 -> x0, other arithmetic: 5.69 us -> none  [the longest x1 4.54 us: partial_attention(): l = jnp.sum(p, axis=2)]
    reshape x1 -> x0, local copies, waits for them, and re-layouts: 1.58 us -> none  [local(): od = od.reshape(b, n, h // n, lat)]
  transfers between devices with their start and end apart: 3 -> 0, of which waited for: 2 -> 0; matrix products, arithmetic and copies ran while one was open for 10% -> 0% of each run, Pallas kernels for 0% -> 0%
where the time goes in v1:
time: 66.7 us; the launch traced here: 65.7 us
  Pallas kernels  64.1 us (96%)
  local copies, waits for them, and re-layouts  1.57 us (2%)
    pallas_call x1, Pallas kernels, local(): pl.pallas_call(functools.partial(kernel, n), out_shape=jax.ShapeDtypeStru...  64.1 us
    unnamed x1, local copies, waits for them, and re-layouts  1.57 us

profile of v1, /device:TPU:21, one launch (start us, length us, event | category | flops | bytes accessed | tf_op | source)
XLA Modules:
  0.0 65.7 jit_solution(6029437933501991989)
XLA Ops:
  0.0 64.1 %mla_decode.1 = bf16[16,8,512]{2,1,0:T(8,128)(2,1)} custom-call(s32[16]{0:T(128)} %len_ref.1, bf16[16,8,576]{2,1,0:T(8,128)(2,1)} %q_ref.1, bf16[16,576,1024]{2,1,0:T(8,128)(2,1)} %bitcast.1), custom_call_target="tpu_custom_call" | custom-call | tf_op jit(solution)/shard_map/mla_decode/pallas_call | solution.py:233
  64.1 1.6 %copy.5 = bf16[16,8,512]{2,1,0:T(8,128)(2,1)} copy(bf16[16,8,512]{2,1,0:T(8,128)(2,1)} %mla_decode.1) | data formatting | bytes 262144
